TPU v7x, 32 devices: a whole 2x2x4 slice. The times are simulated.
32 devices in a mesh: seq: 8 (over z, y), tp: 4 (over x, core).
Axes of the slice: x: 2, y: 2, z: 4, core: 2. Of those that a mesh axis runs over, the one named last changes fastest.
Arguments:
- ssm_inputs: bfloat16 [8192, 8192], P('seq', 'tp'), may hold values from -6 to 6
- step_sizes: float32 [8192, 128], P('seq', 'tp'), as said below
- decay_rates: float32 [128], P('tp'), as said below
- state_inputs: bfloat16 [8192, 128], P('seq'), may hold values from -6 to 6
- state_readout: bfloat16 [8192, 128], P('seq'), may hold values from -0.5 to 0.5
- skip_gain: float32 [128], P('tp'), may hold values from 0.5 to 1.5
- mixed_inputs: bfloat16 [1536, 8192], P('seq', 'tp'), may hold values from -6 to 6
- out_weight: bfloat16 [8192, 8192], P('tp', 'seq'), may hold values from -0.0625 to 0.0625
Outputs:
- ssm_output: bfloat16 [8192, 8192], P('seq', 'tp')
- projected: bfloat16 [1536, 8192], P('seq', 'tp')
Inputs may be any that keep to these rules, and one draw needn't show every extreme that they name: `step_sizes`: all entries are positive. `decay_rates`: all entries are positive.
All inputs are finite; a program needn't handle non-finite values.
Results may differ from a plain program's by a relative error of at most 0.017.
Values may be sent and summed in bfloat16 or wider, within the bound.
A program may use at most 192 MiB of HBM per device.

v0:
```python
import jax
import jax.numpy as jnp
from jax import lax
from jax.sharding import PartitionSpec as P

HEAD_DIM = 64
STATE = 128
SPAN = 256


def carried_in(array, axis, join, neutral):
    place = lax.axis_index(axis)
    gathered = jax.tree.map(
        lambda a, kind: lax.all_gather(a.astype(kind), axis), array, (jnp.bfloat16, jnp.bfloat16)
    )
    state = jax.tree.map(lambda a, e: jnp.zeros_like(a) + jnp.asarray(e, a.dtype), array, neutral)

    def one(lap, state):
        return join(
            state,
            jax.tree.map(
                lambda a, own: lax.dynamic_index_in_dim(a, lap, 0, False).astype(own.dtype),
                gathered,
                array,
            ),
        )

    return lax.fori_loop(0, place, one, state)


def combine(earlier, latter):
    return (earlier[0] * latter[0], latter[0][:, None, None] * earlier[1] + latter[1])


def per_device(
    ssm_inputs,
    step_sizes,
    decay_rates,
    state_inputs,
    state_readout,
    skip_gain,
    mixed_inputs,
    out_weight,
):
    row_count = ssm_inputs.shape[0]
    head_count = step_sizes.shape[1]
    block_count = row_count // SPAN
    x_blocks = ssm_inputs.reshape(block_count, SPAN, head_count, HEAD_DIM)
    dt_blocks = step_sizes.reshape(block_count, SPAN, head_count)
    b_blocks = state_inputs.reshape(block_count, SPAN, STATE)
    c_blocks = state_readout.reshape(block_count, SPAN, STATE)
    log_decay = jnp.cumsum(-decay_rates[None, None, :] * dt_blocks, axis=1)
    block_decay = log_decay[:, -1, :]
    tail_weight = jnp.exp(block_decay[:, None, :] - log_decay) * dt_blocks
    weighted = (tail_weight[..., None] * x_blocks).astype(jnp.bfloat16)
    block_states = jnp.einsum(
        "cshp,csn->chpn", weighted, b_blocks, preferred_element_type=jnp.float32
    )
    carried = jnp.zeros((head_count, HEAD_DIM, STATE), jnp.float32)
    entering = []
    for block_id in range(block_count):
        entering.append(carried)
        carried = jnp.exp(block_decay[block_id])[:, None, None] * carried + block_states[block_id]
    total_decay = jnp.exp(jnp.sum(block_decay, axis=0))
    identity = (jnp.ones_like(total_decay), jnp.zeros_like(carried))
    decay_before, state_before = carried_in((total_decay, carried), "seq", combine, identity)
    prior_decay = jnp.exp(jnp.cumsum(block_decay, axis=0) - block_decay)
    entering_all = jnp.stack(entering) + prior_decay[:, :, None, None] * state_before[None]
    entering_rounded = entering_all.astype(jnp.bfloat16)
    readout = jnp.einsum(
        "ctn,chpn->cthp", c_blocks, entering_rounded, preferred_element_type=jnp.float32
    )
    y_off = jnp.exp(log_decay)[..., None] * readout
    gram = jnp.einsum("ctn,csn->cts", c_blocks, b_blocks, preferred_element_type=jnp.float32)
    per_head = jnp.transpose(log_decay, (0, 2, 1))
    differ = per_head[:, :, :, None] - per_head[:, :, None, :]
    lower = jnp.tril(jnp.ones((SPAN, SPAN), dtype=bool))
    decay = jnp.exp(jnp.where(lower[None, None], differ, -jnp.inf))
    dt_heads = jnp.transpose(dt_blocks, (0, 2, 1))
    scores = (gram[:, None] * decay * dt_heads[:, :, None, :]).astype(jnp.bfloat16)
    y_diag = jnp.einsum("chts,cshp->cthp", scores, x_blocks, preferred_element_type=jnp.float32)
    combined = y_diag + y_off + skip_gain[None, None, :, None] * x_blocks
    ssm_output = combined.astype(jnp.bfloat16).reshape(row_count, head_count * HEAD_DIM)
    spread_rows = jnp.dot(
        lax.all_gather(mixed_inputs, "seq", axis=0, tiled=True),
        out_weight,
        preferred_element_type=jnp.float32,
    )
    regrouped = lax.all_to_all(
        spread_rows.astype(jnp.bfloat16), "seq", split_axis=0, concat_axis=1, tiled=True
    )
    group_terms = regrouped.astype(jnp.float32)
    projected = lax.psum_scatter(
        group_terms.astype(jnp.bfloat16), "tp", scatter_dimension=1, tiled=True
    )
    return (ssm_output, projected)


def solution(mesh):
    in_specs = (
        P("seq", "tp"),
        P("seq", "tp"),
        P("tp"),
        P("seq", None),
        P("seq", None),
        P("tp"),
        P("seq", "tp"),
        P("tp", "seq"),
    )
    out_specs = (P("seq", "tp"), P("seq", "tp"))
    return jax.shard_map(
        per_device, mesh=mesh, in_specs=in_specs, out_specs=out_specs, check_vma=False
    )
```

profile of v0, /device:TPU:28, one launch (start us, length us, event | category | flops | bytes accessed | tf_op | source)
XLA Modules:
  0.0 322.4 jit_solution(16475436109490359027)
XLA Ops:
  7.2 0.0 copy-start
  7.2 0.0 all-gather.6.cloned.1.call-start
  7.2 0.7 all-gather.6.cloned.1.call-update
  7.9 0.0 all-gather.4.cloned.1.call-start
  8.0 1.0 reshape.138
  8.9 0.7 neg.4
  9.6 0.1 multiply_bitcast_fusion
  9.7 0.1 reshape.153
  9.8 2.3 reduce-window.6
  12.2 0.1 slice.52
  12.3 0.1 copy.63
  12.4 12.9 %reshape.155 = bf16[4,256,32,64]{3,2,1,0:T(8,128)(2,1)} reshape(bf16[1024,2048]{1,0:T(8,128)(2,1)} %param.10) | data formatting | bytes 8388608 | tf_op jit(solution)/shard_map/reshape | solution.py:48
  25.3 10.4 %copy.68 = bf16[4,256,32,64]{1,3,2,0:T(8,128)(2,1)} copy(bf16[4,256,32,64]{3,2,1,0:T(8,128)(2,1)} %reshape.155) | data formatting | bytes 8388608 | tf_op jit(solution)/shard_map/reshape | solution.py:48
  35.8 0.1 fusion.29
  35.9 0.2 fusion.20
  36.1 0.2 slice_reduce_fusion
  36.3 0.0 copy-done.2
  36.3 0.1 bitcast_multiply_fusion.1
  36.5 0.0 copy-done.1
  36.5 3.5 %fusion.11 = f32[4,32,64,128]{3,2,1,0:T(8,128)S(1)} fusion(bf16[4,256,128,1]{2,1,3,0:T(8,128)(2,1)S(1)} %bitcast.77, bf16[4,256,32,64]{1,3,2,0:T(8,128)(2,1)} %copy.68, f32[4,256,32]{1,2,0:T(8,128)S(1)} %get-tuple-element.75), kind=kOutput, calls=%fused_computation.17 | convolution fusion | flops 543162368 | bytes 8781824 | tf_op jit(solution)/shard_map/cshp,csn->chpn/dot_general | solution.py:56
  40.0 1.5 fusion.19
  41.5 0.0 all-gather.4.cloned.1.call-update
  41.5 0.0 reduce-scatter.2.cloned.1.call-start
  41.5 65.5 %all-gather.6.cloned.1.call-done = bf16[1536,2048]{1,0:T(8,128)(2,1)} async-done(((bf16[192,2048]{1,0:T(8,128)(2,1)}), bf16[1536,2048]{1,0:T(8,128)(2,1)}) %all-gather.6.cloned.1.call-update) | async-done | bytes 6291472 | tf_op jit(solution)/shard_map/all_gather | solution.py:85
  107.0 10.0 %convolution_convert_fusion = bf16[1536,1024]{1,0:T(8,128)(2,1)S(1)} fusion(bf16[1536,2048]{1,0:T(8,128)(2,1)} %all-gather.6.cloned.1.call-done, bf16[2048,1024]{1,0:T(8,128)(2,1)} %param.17), kind=kOutput, calls=%fused_computation.21 | convolution fusion | flops 6444023808 | bytes 13631488 | tf_op jit(solution)/shard_map/dot_general | solution.py:84
  117.0 121.2 %all_to_all.19 = bf16[8,192,1024]{2,1,0:T(8,128)(2,1)S(1)} all-to-all(bf16[8,192,1024]{2,1,0:T(8,128)(2,1)S(1)} %bitcast.76), channel_id=1, replica_groups=mesh['seq'=8,'tp'=4] {'seq'}, dimensions={0} | all-to-all | bytes 6291456 | tf_op jit(solution)/shard_map/all_to_all | solution.py:89
  238.2 2.1 copy.84
  240.3 0.0 reduce-scatter.2.cloned.1.call-update
  240.4 0.0 copy-done.4
  240.4 0.6 dynamic-slice
  241.6 0.2 dynamic-update-slice
  241.8 16.9 %all-reduce = bf16[256]{0:T(256)(128)(2,1)S(1)} all-reduce(bf16[256]{0:T(256)(128)(2,1)S(1)} %dynamic-update-slice), channel_id=2, replica_groups=mesh['seq'=8,'tp'=4] {'seq'}, use_global_device_ids=true, to_apply=%add | all-reduce | flops 256 | bytes 1024
  258.7 0.1 reshape.145
  258.9 0.3 fusion.30
  259.2 12.6 %fusion = f32[4,32,256,64]{2,3,1,0:T(8,128)} fusion(bf16[4,256,32,64]{1,3,2,0:T(8,128)(2,1)} %copy.68, f32[4,32,256]{2,1,0:T(8,128)S(1)} %copy.66, f32[4,32,256]{2,1,0:T(8,128)S(1)} %get-tuple-element.78, f32[4,256,256]{2,1,0:T(8,128)S(1)} %fusion.30, pred[256,256]{1,0:T(8,128)(4,1)S(1)} %iota_compare_fusion), kind=kOutput, calls=%fused_computation.3 | convolution fusion | flops 1115684864 | bytes 13959168 | tf_op jit(solution)/shard_map/chts,cshp->cthp/dot_general | solution.py:81
  271.8 0.1 broadcast.34
  271.9 0.0 copy-start.3
  271.9 9.7 %while.12 = (s32[]{:T(128)}, f32[32,64,128]{2,1,0:T(8,128)S(1)}, s32[]{:T(128)}, bf16[8,32]{1,0:T(8,128)(2,1)S(1)}, bf16[8,32,64,128]{3,2,1,0:T(8,128)(2,1)}, /*index=5*/s32[]{:T(128)}, s32[]{:T(128)}, s32[]{:T(128)}) while((s32[]{:T(128)}, f32[32,64,128]{2,1,0:T(8,128)S(1)}, s32[]{:T(128)}, bf16[8,32]{1,0:T(8,128)(2,1)S(1)}, ...), condition=%wide.region_5.6_spmd, body=%wide.region_4.5_spmd.sunk | while | flops 786469 | bytes 2621887 | solution.py:28
  272.0 1.3 convert_add_fusion.2
  273.3 1.3 convert_add_fusion.2
  274.7 1.3 convert_add_fusion.2
  276.0 1.3 convert_add_fusion.2
  277.4 1.3 convert_add_fusion.2
  278.7 1.3 convert_add_fusion.2
  280.1 1.3 convert_add_fusion.2
  281.6 9.0 %fusion.9 = bf16[4,256,32,64]{1,3,2,0:T(8,128)(2,1)} fusion(bf16[4,256,32,64]{1,3,2,0:T(8,128)(2,1)} %copy.68, f32[4,32,256,64]{2,3,1,0:T(8,128)} %fusion, f32[32]{0:T(128)S(1)} %copy-done.3, f32[4,256,32]{1,2,0:T(8,128)S(1)} %get-tuple-element.76, bf16[4,256,128,1]{2,1,3,0:T(8,128)(2,1)S(1)} %bitcast.73, f32[1,32,64,128]{3,2,1,0:T(8,128)S(1)} %get-tuple-element.72, ...), kind=kOutput, calls=%fused_computation.14 | convolution fusion | flops 555745280 | bytes 21365392 | tf_op jit(solution)/shard_map/ctn,chpn->cthp/dot_general | solution.py:70
  290.7 12.9 %copy.78 = bf16[4,256,32,64]{3,2,1,0:T(8,128)(2,1)} copy(bf16[4,256,32,64]{1,3,2,0:T(8,128)(2,1)} %fusion.9) | data formatting | bytes 8388608
  303.6 12.3 %reshape.154 = bf16[1024,2048]{1,0:T(8,128)(2,1)} reshape(bf16[4,256,32,64]{3,2,1,0:T(8,128)(2,1)} %copy.78) | data formatting | bytes 8388608
  (25 shorter events, 0.2 us)
Async XLA Ops:
  7.2 251.7 %copy-start = (bf16[1024,128]{1,0:T(8,128)(2,1)S(1)}, bf16[1024,128]{1,0:T(8,128)(2,1)}, u32[]{:S(2)}) copy-start(bf16[1024,128]{1,0:T(8,128)(2,1)} %param.14) | copy-start | bytes 786436
  7.2 99.8 %all-gather.6.cloned.1.call-start = ((), (), s32[]{:S(2)}) async-start(), calls=%async_computation.3 | async-start | bytes 7077888 | tf_op jit(solution)/shard_map/all_gather | solution.py:85
  7.9 263.9 %all-gather.4.cloned.1.call-start = ((), (), s32[]{:S(2)}) async-start(), calls=%async_computation.2 | async-start | bytes 4718592 | tf_op jit(solution)/shard_map/all_gather | solution.py:14
  25.3 11.0 %copy-start.2 = (f32[1024,32]{0,1:T(8,128)S(1)}, f32[1024,32]{0,1:T(8,128)}, u32[]{:S(2)}) copy-start(f32[1024,32]{0,1:T(8,128)} %param.11) | copy-start | bytes 393220
  25.3 11.1 %copy-start.1 = (bf16[1024,128]{1,0:T(8,128)(2,1)S(1)}, bf16[1024,128]{1,0:T(8,128)(2,1)}, u32[]{:S(2)}) copy-start(bf16[1024,128]{1,0:T(8,128)(2,1)} %param.13) | copy-start | bytes 786436
  41.5 274.4 %reduce-scatter.2.cloned.1.call-start = ((), (), s32[]{:S(2)}) async-start(), calls=%async_computation.4 | async-start | bytes 3932160 | tf_op jit(solution)/shard_map/reduce_scatter | solution.py:93
  238.2 2.2 copy-start.4
  271.9 9.7 %copy-start.3 = (f32[32]{0:T(128)S(1)}, f32[32]{0:T(128)}, u32[]{:S(2)}) copy-start(f32[32]{0:T(128)} %param.15) | copy-start | bytes 388
Sparse Core Ops, SparseCore 0:
  10.2 96.8 all-gather.5
  109.1 121.5 all-gather.3
  240.5 38.6 reduce-scatter.1
where the time goes:
time: 324 us; the launch traced here: 322 us
  blocking collectives  138 us (43%)
  waiting for transfers between devices  66.2 us (20%)
  local copies, waits for them, and re-layouts  53.1 us (16%)
  matrix products  35.4 us (11%)
  other arithmetic  14.5 us (4%)
  between operations  14.5 us (4%)
    all_to_all x1, blocking collectives, per_device(): lax.all_to_all(spread_rows.astype(jnp.bfloat16), 'seq', split_axis=0, con...  121 us
    all_gather x1, waiting for transfers between devices, per_device(): lax.all_gather(mixed_inputs, 'seq', axis=0, tiled=True)  65.5 us
    unnamed x15, local copies, waits for them, and re-layouts  26.1 us
    reshape x2, local copies, waits for them, and re-layouts, per_device(): x_blocks = ssm_inputs.reshape(block_count, SPAN, head_count, HEAD_DIM)  23.4 us
    unnamed x1, blocking collectives  16.9 us
    dot_general x1, matrix products, per_device(): jnp.einsum('chts,cshp->cthp', scores, x_blocks, preferred_element_type=jn...  12.6 us
    dot_general x1, matrix products, per_device(): jnp.dot(lax.all_gather(mixed_inputs, 'seq', axis=0, tiled=True), out_weig...  10 us
    add x7, other arithmetic, combine(): latter[0][:, None, None] * earlier[1] + latter[1]  9.14 us
  transfers between devices with their start and end apart: 3, of which 1 were waited for; matrix products, arithmetic and copies ran while one was open for 32% of the time, Pallas kernels for 0%

commit v1 on v0

--- a/solution.py
+++ b/solution.py
@@ -86,8 +86,15 @@
         out_weight,
         preferred_element_type=jnp.float32,
     )
-    regrouped = lax.all_to_all(
-        spread_rows.astype(jnp.bfloat16), "seq", split_axis=0, concat_axis=1, tiled=True
+    in_array = spread_rows.astype(jnp.bfloat16)
+    regrouped = jnp.concatenate(
+        lax.all_to_all(
+            jnp.stack(jnp.split(in_array, lax.axis_size("seq"), 0)),
+            axis_name="seq",
+            split_axis=0,
+            concat_axis=0,
+        ),
+        axis=1,
     )
     group_terms = regrouped.astype(jnp.float32)
     projected = lax.psum_scatter(

time: 324 us -> 324 us (level)
    unnamed x15 -> x22, local copies, waits for them, and re-layouts: 26.1 us -> 26.3 us
where the time goes in v1:
time: 324 us; the launch traced here: 322 us
  blocking collectives  138 us (43%)
  waiting for transfers between devices  66.2 us (20%)
  local copies, waits for them, and re-layouts  53.3 us (16%)
  matrix products  35.4 us (11%)
  between operations  14.6 us (5%)
  other arithmetic  14.5 us (4%)
    all_to_all x1, blocking collectives, per_device(): lax.all_to_all(jnp.stack(jnp.split(in_array, lax.axis_size('seq'), 0)), a...  121 us
    all_gather x1, waiting for transfers between devices, per_device(): lax.all_gather(mixed_inputs, 'seq', axis=0, tiled=True)  65.5 us
    unnamed x22, local copies, waits for them, and re-layouts  26.3 us
    reshape x2, local copies, waits for them, and re-layouts, per_device(): x_blocks = ssm_inputs.reshape(block_count, SPAN, head_count, HEAD_DIM)  23.4 us
    unnamed x1, blocking collectives  16.9 us
    dot_general x1, matrix products, per_device(): jnp.einsum('chts,cshp->cthp', scores, x_blocks, preferred_element_type=jn...  12.6 us
    dot_general x1, matrix products, per_device(): jnp.dot(lax.all_gather(mixed_inputs, 'seq', axis=0, tiled=True), out_weig...  10 us
    add x7, other arithmetic, combine(): latter[0][:, None, None] * earlier[1] + latter[1]  9.14 us
  transfers between devices with their start and end apart: 3, of which 1 were waited for; matrix products, arithmetic and copies ran while one was open for 32% of the time, Pallas kernels for 0%

profile of v1, /device:TPU:28, one launch (start us, length us, event | category | flops | bytes accessed | tf_op | source)
XLA Modules:
  0.0 322.4 jit_solution(15978366350210241653)
XLA Ops:
  7.2 0.0 copy-start
  7.2 0.0 all-gather.6.cloned.1.call-start
  7.2 0.7 all-gather.6.cloned.1.call-update
  7.9 0.0 all-gather.4.cloned.1.call-start
  8.0 1.0 reshape.141
  8.9 0.7 neg.4
  9.6 0.1 multiply_bitcast_fusion
  9.7 0.1 reshape.158
  9.8 2.3 reduce-window.6
  12.2 0.1 slice.52
  12.3 0.1 copy.62
  12.4 12.9 %reshape.160 = bf16[4,256,32,64]{3,2,1,0:T(8,128)(2,1)} reshape(bf16[1024,2048]{1,0:T(8,128)(2,1)} %param.10) | data formatting | bytes 8388608 | tf_op jit(solution)/shard_map/reshape | solution.py:48
  25.3 10.4 %copy.67 = bf16[4,256,32,64]{1,3,2,0:T(8,128)(2,1)} copy(bf16[4,256,32,64]{3,2,1,0:T(8,128)(2,1)} %reshape.160) | data formatting | bytes 8388608 | tf_op jit(solution)/shard_map/reshape | solution.py:48
  35.8 0.1 fusion.37
  35.9 0.2 fusion.28
  36.1 0.2 slice_reduce_fusion
  36.3 0.0 copy-done.2
  36.3 0.1 bitcast_multiply_fusion.1
  36.5 0.0 copy-done.1
  36.5 3.5 %fusion.11 = f32[4,32,64,128]{3,2,1,0:T(8,128)S(1)} fusion(bf16[4,256,128,1]{2,1,3,0:T(8,128)(2,1)S(1)} %bitcast.107, bf16[4,256,32,64]{1,3,2,0:T(8,128)(2,1)} %copy.67, f32[4,256,32]{1,2,0:T(8,128)S(1)} %get-tuple-element.75), kind=kOutput, calls=%fused_computation.17 | convolution fusion | flops 543162368 | bytes 8781824 | tf_op jit(solution)/shard_map/cshp,csn->chpn/dot_general | solution.py:56
  40.0 1.5 fusion.19
  41.5 0.0 all-gather.4.cloned.1.call-update
  41.5 0.0 reduce-scatter.2.cloned.1.call-start
  41.5 65.5 %all-gather.6.cloned.1.call-done = bf16[1536,2048]{1,0:T(8,128)(2,1)} async-done(((bf16[192,2048]{1,0:T(8,128)(2,1)}), bf16[1536,2048]{1,0:T(8,128)(2,1)}) %all-gather.6.cloned.1.call-update) | async-done | bytes 6291472 | tf_op jit(solution)/shard_map/all_gather | solution.py:85
  107.0 10.0 %convolution_convert_fusion = bf16[1536,1024]{1,0:T(8,128)(2,1)S(1)} fusion(bf16[1536,2048]{1,0:T(8,128)(2,1)} %all-gather.6.cloned.1.call-done, bf16[2048,1024]{1,0:T(8,128)(2,1)} %param.17), kind=kOutput, calls=%fused_computation.21 | convolution fusion | flops 6444023808 | bytes 13631488 | tf_op jit(solution)/shard_map/dot_general | solution.py:84
  117.3 120.9 %all_to_all.5 = bf16[8,192,1024]{2,1,0:T(8,128)(2,1)S(1)} all-to-all(bf16[8,192,1024]{2,1,0:T(8,128)(2,1)S(1)} %fusion.20), channel_id=1, replica_groups=mesh['seq'=8,'tp'=4] {'seq'}, dimensions={0} | all-to-all | bytes 6291456 | tf_op jit(solution)/shard_map/all_to_all | solution.py:91
  238.2 2.1 copy.83
  240.3 0.0 reduce-scatter.2.cloned.1.call-update
  240.4 0.0 copy-done.4
  240.4 0.6 dynamic-slice
  241.5 0.2 dynamic-update-slice
  241.8 16.9 %all-reduce = bf16[256]{0:T(256)(128)(2,1)S(1)} all-reduce(bf16[256]{0:T(256)(128)(2,1)S(1)} %dynamic-update-slice), channel_id=2, replica_groups=mesh['seq'=8,'tp'=4] {'seq'}, use_global_device_ids=true, to_apply=%add | all-reduce | flops 256 | bytes 1024
  258.7 0.1 reshape.150
  258.9 0.3 fusion.38
  259.2 12.6 %fusion = f32[4,32,256,64]{2,3,1,0:T(8,128)} fusion(bf16[4,256,32,64]{1,3,2,0:T(8,128)(2,1)} %copy.67, f32[4,32,256]{2,1,0:T(8,128)S(1)} %copy.65, f32[4,32,256]{2,1,0:T(8,128)S(1)} %get-tuple-element.78, f32[4,256,256]{2,1,0:T(8,128)S(1)} %fusion.38, pred[256,256]{1,0:T(8,128)(4,1)S(1)} %iota_compare_fusion), kind=kOutput, calls=%fused_computation.3 | convolution fusion | flops 1115684864 | bytes 13959168 | tf_op jit(solution)/shard_map/chts,cshp->cthp/dot_general | solution.py:81
  271.8 0.1 broadcast.34
  271.9 0.0 copy-start.3
  271.9 9.7 %while.12 = (s32[]{:T(128)}, f32[32,64,128]{2,1,0:T(8,128)S(1)}, s32[]{:T(128)}, bf16[8,32]{1,0:T(8,128)(2,1)S(1)}, bf16[8,32,64,128]{3,2,1,0:T(8,128)(2,1)}, /*index=5*/s32[]{:T(128)}, s32[]{:T(128)}, s32[]{:T(128)}) while((s32[]{:T(128)}, f32[32,64,128]{2,1,0:T(8,128)S(1)}, s32[]{:T(128)}, bf16[8,32]{1,0:T(8,128)(2,1)S(1)}, ...), condition=%wide.region_5.6_spmd, body=%wide.region_4.5_spmd.sunk | while | flops 786469 | bytes 2621887 | solution.py:28
  272.0 1.3 convert_add_fusion.2
  273.3 1.3 convert_add_fusion.2
  274.7 1.3 convert_add_fusion.2
  276.0 1.3 convert_add_fusion.2
  277.4 1.3 convert_add_fusion.2
  278.7 1.3 convert_add_fusion.2
  280.1 1.3 convert_add_fusion.2
  281.6 9.0 %fusion.9 = bf16[4,256,32,64]{1,3,2,0:T(8,128)(2,1)} fusion(bf16[4,256,32,64]{1,3,2,0:T(8,128)(2,1)} %copy.67, f32[4,32,256,64]{2,3,1,0:T(8,128)} %fusion, f32[32]{0:T(128)S(1)} %copy-done.3, f32[4,256,32]{1,2,0:T(8,128)S(1)} %get-tuple-element.76, bf16[4,256,128,1]{2,1,3,0:T(8,128)(2,1)S(1)} %bitcast.104, f32[1,32,64,128]{3,2,1,0:T(8,128)S(1)} %get-tuple-element.72, ...), kind=kOutput, calls=%fused_computation.14 | convolution fusion | flops 555745280 | bytes 21365392 | tf_op jit(solution)/shard_map/ctn,chpn->cthp/dot_general | solution.py:70
  290.6 12.9 %copy.77 = bf16[4,256,32,64]{3,2,1,0:T(8,128)(2,1)} copy(bf16[4,256,32,64]{1,3,2,0:T(8,128)(2,1)} %fusion.9) | data formatting | bytes 8388608
  303.6 12.3 %reshape.159 = bf16[1024,2048]{1,0:T(8,128)(2,1)} reshape(bf16[4,256,32,64]{3,2,1,0:T(8,128)(2,1)} %copy.77) | data formatting | bytes 8388608
  (33 shorter events, 0.4 us)
Async XLA Ops:
  7.2 251.7 %copy-start = (bf16[1024,128]{1,0:T(8,128)(2,1)S(1)}, bf16[1024,128]{1,0:T(8,128)(2,1)}, u32[]{:S(2)}) copy-start(bf16[1024,128]{1,0:T(8,128)(2,1)} %param.14) | copy-start | bytes 786436
  7.2 99.8 %all-gather.6.cloned.1.call-start = ((), (), s32[]{:S(2)}) async-start(), calls=%async_computation.3 | async-start | bytes 7077888 | tf_op jit(solution)/shard_map/all_gather | solution.py:85
  7.9 263.9 %all-gather.4.cloned.1.call-start = ((), (), s32[]{:S(2)}) async-start(), calls=%async_computation.2 | async-start | bytes 4718592 | tf_op jit(solution)/shard_map/all_gather | solution.py:14
  25.3 11.0 %copy-start.2 = (f32[1024,32]{0,1:T(8,128)S(1)}, f32[1024,32]{0,1:T(8,128)}, u32[]{:S(2)}) copy-start(f32[1024,32]{0,1:T(8,128)} %param.11) | copy-start | bytes 393220
  25.3 11.1 %copy-start.1 = (bf16[1024,128]{1,0:T(8,128)(2,1)S(1)}, bf16[1024,128]{1,0:T(8,128)(2,1)}, u32[]{:S(2)}) copy-start(bf16[1024,128]{1,0:T(8,128)(2,1)} %param.13) | copy-start | bytes 786436
  41.5 274.4 %reduce-scatter.2.cloned.1.call-start = ((), (), s32[]{:S(2)}) async-start(), calls=%async_computation.4 | async-start | bytes 3932160 | tf_op jit(solution)/shard_map/reduce_scatter | solution.py:100
  238.2 2.2 copy-start.4
  271.9 9.7 %copy-start.3 = (f32[32]{0:T(128)S(1)}, f32[32]{0:T(128)}, u32[]{:S(2)}) copy-start(f32[32]{0:T(128)} %param.15) | copy-start | bytes 388
Sparse Core Ops, SparseCore 0:
  10.2 96.8 all-gather.5
  109.1 121.4 all-gather.3
  240.5 38.6 reduce-scatter.1
